TPU v7x, 32 devices: a whole 2x2x4 slice. The times are simulated.
32 devices in a mesh: dev: 32 (over z, y, x, core).
Axes of the slice: x: 2, y: 2, z: 4, core: 2. Of those that a mesh axis runs over, the one named last changes fastest.
Arguments:
- tokens: bfloat16 [4608, 1536], P('dev'), may hold values from -6 to 6
- conditioning: bfloat16 [4, 1536], replicated, may hold values from -5 to 5
- text_lengths: int32 [4], replicated, may hold values from 86 to 154, as said below
- modulation_weight: bfloat16 [3072, 9216], P('dev'), may hold values from -0.15625 to 0.15625
- project_weight: bfloat16 [3072, 4608], P('dev'), may hold values from -1 to 1
- merge_weight: bfloat16 [3072, 1536], P('dev'), may hold values from -1.25 to 1.25
- up_weight: bfloat16 [3072, 6144], P('dev'), may hold values from -0.15625 to 0.15625
- down_weight: bfloat16 [12288, 1536], P('dev'), may hold values from -0.078125 to 0.078125
- cotangent: bfloat16 [4608, 1536], P('dev'), may hold values from -6 to 6
Outputs:
- layer_out: bfloat16 [4608, 1536], P('dev')
- tokens_grad: float32 [4608, 1536], P('dev')
- conditioning_grad: float32 [4, 1536], replicated
- modulation_grad: float32 [3072, 9216], P('dev')
- project_grad: float32 [3072, 4608], P('dev')
- merge_grad: float32 [3072, 1536], P('dev')
- up_grad: float32 [3072, 6144], P('dev')
- down_grad: float32 [12288, 1536], P('dev')
Inputs may be any that keep to these rules, and one draw needn't show every extreme that they name: `text_lengths`: the text tokens of all sequences sum to 512, so that the sequences fill the packed rows exactly; one sequence has exactly 154 text tokens.
All inputs are finite; a program needn't handle non-finite values.
Results may differ from a plain program's by a relative error of at most 0.025.
The roundings to bfloat16 on the way count: a program that leaves them out, or rounds other values in their place, can miss the bound.
Values may be sent and summed in bfloat16 or wider, within the bound.
A program may use at most 576 MiB of HBM per device.

v0:
```python
import jax
import jax.numpy as jnp
from jax import lax
from jax.sharding import PartitionSpec as P

HEADS = 24
HDIM = 64
IMG = 1024
REACH = 9
TXT_CAP = 144
HIGHEST_PRECISION = lax.Precision.HIGHEST
EPSILON = 1e-06
CONTRACT_LAST = (((1,), (1,)), ((), ()))
CONTRACT_FIRST = (((0,), (0,)), ((), ()))


def passed_along(x, axis, by):
    length = lax.axis_size(axis)
    pairs = [(i, i + by) for i in range(length) if 0 <= i + by < length]
    return lax.ppermute(x, axis, pairs)


def layer_norm(values):
    mean = jnp.mean(values, axis=-1, keepdims=True)
    centred = values - mean
    variance = jnp.mean(centred * centred, axis=-1, keepdims=True)
    inv_std = lax.rsqrt(variance + EPSILON)
    return (centred * inv_std, inv_std)


def norm_back(grad_normed, normed, inv_std):
    mean_grad = jnp.mean(grad_normed, axis=-1, keepdims=True)
    mean_cross = jnp.mean(grad_normed * normed, axis=-1, keepdims=True)
    return inv_std * (grad_normed - mean_grad - normed * mean_cross)


def sequence_index(positions, starts):
    return jnp.sum((starts[None, :] <= positions[:, None]).astype(jnp.int32), axis=1) - 1


def stream_dot(rows, stacked, layout):
    text_rows, text_valid, slot_of_row, is_text = layout
    half = stacked.shape[0] // 2
    image_part = jnp.dot(rows, stacked[:half], preferred_element_type=jnp.float32)
    text_part = jnp.dot(rows[text_rows], stacked[half:], preferred_element_type=jnp.float32)
    return jnp.where(is_text[:, None], text_part[slot_of_row], image_part)


def stream_rows_back(stacked, grad_low, layout):
    text_rows, text_valid, slot_of_row, is_text = layout
    half = stacked.shape[0] // 2
    image_grad = jnp.where(is_text[:, None], jnp.zeros_like(grad_low), grad_low)
    picked = grad_low[text_rows]
    text_grad = jnp.where(text_valid[:, None], picked, jnp.zeros_like(picked))
    image_back = lax.dot_general(
        image_grad, stacked[:half], CONTRACT_LAST, preferred_element_type=jnp.float32
    )
    text_back = lax.dot_general(
        text_grad, stacked[half:], CONTRACT_LAST, preferred_element_type=jnp.float32
    )
    return jnp.where(is_text[:, None], text_back[slot_of_row], image_back)


def split_streams(rows, is_text):
    zeros = jnp.zeros_like(rows)
    return jnp.concatenate(
        [jnp.where(is_text[:, None], zeros, rows), jnp.where(is_text[:, None], rows, zeros)], axis=1
    )


def term_rows(stacked_rows, grad_low):
    return lax.dot_general(
        stacked_rows, grad_low, CONTRACT_FIRST, preferred_element_type=jnp.float32
    )


def gather_tail(merge_weight, up_weight, down_weight):
    return (
        lax.all_gather(merge_weight, "dev", axis=0, tiled=True),
        lax.all_gather(up_weight, "dev", axis=0, tiled=True),
        lax.all_gather(down_weight, "dev", axis=0, tiled=True),
    )


def heads_last(stacked, count):
    return jnp.transpose(stacked, (1, 0, 2)).reshape(count, HEADS * HDIM)


def on_device(
    tokens,
    conditioning,
    text_lengths,
    modulation_weight,
    project_weight,
    merge_weight,
    up_weight,
    down_weight,
    cotangent,
):
    rows_dev = tokens.shape[0]
    width = tokens.shape[1]
    shard_rows = modulation_weight.shape[0]
    seq_count = conditioning.shape[0]
    devices = lax.axis_size("dev")
    device = lax.axis_index("dev")
    window = (2 * REACH + 1) * rows_dev
    scale = HDIM ** (-0.5)
    own_stream = device * shard_rows // width
    feature_start = device * shard_rows % width
    lengths = IMG + text_lengths
    ends = jnp.cumsum(lengths)
    starts = jnp.concatenate([jnp.zeros((1,), jnp.int32), ends[:-1]])
    positions = device * rows_dev + jnp.arange(rows_dev, dtype=jnp.int32)
    row_seq = sequence_index(positions, starts)
    row_start = jnp.max(
        jnp.where(starts[None, :] <= positions[:, None], starts[None, :], 0), axis=1
    )
    is_text = positions - row_start >= IMG
    text_count = jnp.cumsum(is_text.astype(jnp.int32))
    slot_of_row = jnp.clip(text_count - 1, 0, TXT_CAP - 1)
    slot_range = jnp.arange(TXT_CAP, dtype=jnp.int32)
    text_rows = jnp.clip(
        jnp.sum((text_count[None, :] <= slot_range[:, None]).astype(jnp.int32), axis=1),
        0,
        rows_dev - 1,
    )
    text_valid = slot_range < text_count[-1]
    layout = (text_rows, text_valid, slot_of_row, is_text)
    codes = row_seq * 2 + is_text.astype(jnp.int32)
    one_hot = (codes[:, None] == jnp.arange(2 * seq_count, dtype=jnp.int32)[None, :]).astype(
        jnp.float32
    )
    key_positions = device * rows_dev - REACH * rows_dev + jnp.arange(window, dtype=jnp.int32)
    key_valid = (key_positions >= 0) & (key_positions < devices * rows_dev)
    key_seq = sequence_index(key_positions, starts)
    mask = (row_seq[:, None] == key_seq[None, :]) & key_valid[None, :]
    cond_float = conditioning.astype(jnp.float32)
    silu_low = jax.nn.silu(cond_float).astype(jnp.bfloat16)
    silu_part = lax.dynamic_slice_in_dim(silu_low, feature_start, shard_rows, 1)
    mod_full, project_full = (
        lax.all_gather(modulation_weight, "dev", axis=0, tiled=True),
        lax.all_gather(project_weight, "dev", axis=0, tiled=True),
    )
    mod_table = jnp.einsum(
        "sd,jdc->sjc",
        silu_low,
        mod_full.reshape(2, width, 6 * width),
        preferred_element_type=jnp.float32,
    )
    mod_rows = jnp.dot(
        one_hot,
        mod_table.reshape(2 * seq_count, 6 * width),
        precision=HIGHEST_PRECISION,
        preferred_element_type=jnp.float32,
    )
    shift_a, scale_a, gate_a, shift_b, scale_b, gate_b = jnp.split(mod_rows, 6, axis=1)
    inputs = tokens.astype(jnp.float32)
    normed_a, inv_a = layer_norm(inputs)
    hidden_a = (normed_a * (1.0 + scale_a) + shift_a).astype(jnp.bfloat16)
    projected = stream_dot(hidden_a, project_full, layout).astype(jnp.bfloat16)
    queries, keys, values = jnp.split(projected, 3, axis=1)
    key_pieces = []
    value_pieces = []
    for offset in range(-REACH, REACH + 1):
        if offset == 0:
            key_pieces.append(keys)
            value_pieces.append(values)
        else:
            got_keys, got_values = passed_along((keys, values), "dev", -offset)
            key_pieces.append(got_keys)
            value_pieces.append(got_values)
    window_keys = jnp.concatenate(key_pieces, axis=0)
    window_values = jnp.concatenate(value_pieces, axis=0)

    def head_forward(head):
        query = lax.dynamic_slice_in_dim(queries, head * HDIM, HDIM, 1)
        key_cols = lax.dynamic_slice_in_dim(window_keys, head * HDIM, HDIM, 1)
        value_cols = lax.dynamic_slice_in_dim(window_values, head * HDIM, HDIM, 1)
        scores = (
            lax.dot_general(query, key_cols, CONTRACT_LAST, preferred_element_type=jnp.float32)
            * scale
        )
        masked = jnp.where(mask, scores, -jnp.inf)
        top = jnp.max(masked, axis=1, keepdims=True)
        exponent = jnp.exp(masked - top)
        total = jnp.sum(exponent, axis=1, keepdims=True)
        probs = (exponent / total).astype(jnp.bfloat16)
        attended_head = jnp.dot(probs, value_cols, preferred_element_type=jnp.float32)
        return (attended_head, (top + jnp.log(total))[:, 0])

    head_out, log_totals = lax.map(head_forward, jnp.arange(HEADS, dtype=jnp.int32))
    attended = heads_last(head_out, rows_dev).astype(jnp.bfloat16)
    merge_full, up_full, down_full = gather_tail(merge_weight, up_weight, down_weight)
    merged = stream_dot(attended, merge_full, layout)
    middle = inputs + gate_a * merged
    normed_b, inv_b = layer_norm(middle)
    hidden_b = (normed_b * (1.0 + scale_b) + shift_b).astype(jnp.bfloat16)
    upper = stream_dot(hidden_b, up_full, layout)
    activated = jax.nn.gelu(upper, approximate=True).astype(jnp.bfloat16)
    lowered = stream_dot(activated, down_full, layout)
    layer_out = (middle + gate_b * lowered).astype(jnp.bfloat16)
    grad_out = cotangent.astype(jnp.float32)
    grad_gate_b = grad_out * lowered
    grad_lowered = (gate_b * grad_out).astype(jnp.bfloat16)
    merge_again, up_again, down_again = gather_tail(merge_weight, up_weight, down_weight)
    grad_activated = stream_rows_back(down_again, grad_lowered, layout)
    activated_split = split_streams(activated, is_text)
    down_grad = lax.psum_scatter(
        term_rows(activated_split, grad_lowered), "dev", scatter_dimension=0, tiled=True
    )
    gelu_pull = jax.vjp(lambda value_in: jax.nn.gelu(value_in, approximate=True), upper)[1]
    grad_upper = gelu_pull(grad_activated)[0].astype(jnp.bfloat16)
    grad_hidden_b = stream_rows_back(up_again, grad_upper, layout)
    grad_scale_b = grad_hidden_b * normed_b
    grad_middle = grad_out + norm_back(grad_hidden_b * (1.0 + scale_b), normed_b, inv_b)
    grad_gate_a = grad_middle * merged
    grad_merged = (gate_a * grad_middle).astype(jnp.bfloat16)
    grad_attended = stream_rows_back(merge_again, grad_merged, layout).astype(jnp.bfloat16)
    attended_split = split_streams(attended, is_text)
    hidden_b_split = split_streams(hidden_b, is_text)

    def head_backward(head):
        query = lax.dynamic_slice_in_dim(queries, head * HDIM, HDIM, 1)
        key_cols = lax.dynamic_slice_in_dim(window_keys, head * HDIM, HDIM, 1)
        value_cols = lax.dynamic_slice_in_dim(window_values, head * HDIM, HDIM, 1)
        grad_head = lax.dynamic_slice_in_dim(grad_attended, head * HDIM, HDIM, 1)
        log_total = log_totals[head]
        scores = (
            lax.dot_general(query, key_cols, CONTRACT_LAST, preferred_element_type=jnp.float32)
            * scale
        )
        probs = jnp.where(mask, jnp.exp(scores - log_total[:, None]), 0.0)
        grad_probs = lax.dot_general(
            grad_head, value_cols, CONTRACT_LAST, preferred_element_type=jnp.float32
        )
        inner = jnp.sum(probs * grad_probs, axis=1, keepdims=True)
        grad_scores = (probs * (grad_probs - inner)).astype(jnp.bfloat16)
        grad_query = jnp.dot(grad_scores, key_cols, preferred_element_type=jnp.float32) * scale
        grad_key = (
            lax.dot_general(grad_scores, query, CONTRACT_FIRST, preferred_element_type=jnp.float32)
            * scale
        )
        grad_value = lax.dot_general(
            probs.astype(jnp.bfloat16),
            grad_head,
            CONTRACT_FIRST,
            preferred_element_type=jnp.float32,
        )
        return (grad_query, grad_key, grad_value)

    head_queries, head_keys, head_values = lax.map(
        head_backward, jnp.arange(HEADS, dtype=jnp.int32)
    )
    grad_queries = heads_last(head_queries, rows_dev)
    grad_keys = heads_last(head_keys, window)
    grad_values = heads_last(head_values, window)
    centre = REACH * rows_dev
    key_total = grad_keys[centre : centre + rows_dev]
    value_total = grad_values[centre : centre + rows_dev]
    for offset in range(-REACH, REACH + 1):
        if offset != 0:
            block = (offset + REACH) * rows_dev
            got_key, got_value = (
                passed_along(
                    grad_keys[block : block + rows_dev].astype(jnp.bfloat16), "dev", offset
                ).astype(jnp.float32),
                passed_along(
                    grad_values[block : block + rows_dev].astype(jnp.bfloat16), "dev", offset
                ).astype(jnp.float32),
            )
            key_total = key_total + got_key
            value_total = value_total + got_value
    grad_projected = jnp.concatenate([grad_queries, key_total, value_total], axis=1).astype(
        jnp.bfloat16
    )
    project_again = lax.all_gather(project_weight, "dev", axis=0, tiled=True)
    grad_hidden_a = stream_rows_back(project_again, grad_projected, layout)
    hidden_a_split = split_streams(hidden_a, is_text)
    summed = lax.psum_scatter(
        jnp.concatenate(
            [
                term_rows(attended_split, grad_merged),
                term_rows(hidden_b_split, grad_upper),
                term_rows(hidden_a_split, grad_projected),
            ],
            axis=1,
        ),
        "dev",
        scatter_dimension=0,
        tiled=True,
    )
    merge_grad = summed[:, :width]
    up_grad = summed[:, width : width + up_weight.shape[1]]
    project_grad = summed[:, width + up_weight.shape[1] :]
    grad_scale_a = grad_hidden_a * normed_a
    tokens_grad = grad_middle + norm_back(grad_hidden_a * (1.0 + scale_a), normed_a, inv_a)
    grad_mod_rows = jnp.concatenate(
        [grad_hidden_a, grad_scale_a, grad_gate_a, grad_hidden_b, grad_scale_b, grad_gate_b], axis=1
    )
    local_table = lax.dot_general(
        one_hot,
        grad_mod_rows,
        CONTRACT_FIRST,
        precision=HIGHEST_PRECISION,
        preferred_element_type=jnp.float32,
    )
    grad_table = lax.psum(local_table.reshape(seq_count, 2, 6 * width), "dev").astype(jnp.bfloat16)
    own_grads = lax.dynamic_index_in_dim(grad_table, own_stream, 1, keepdims=False)
    modulation_grad = lax.dot_general(
        silu_part, own_grads, CONTRACT_FIRST, preferred_element_type=jnp.float32
    )
    grad_piece = lax.dot_general(
        own_grads, modulation_weight, CONTRACT_LAST, preferred_element_type=jnp.float32
    )
    gathered = lax.all_gather(grad_piece, "dev", axis=1, tiled=True)
    grad_silu = gathered[:, :width] + gathered[:, width:]
    silu_pull = jax.vjp(jax.nn.silu, cond_float)[1]
    conditioning_grad = silu_pull(grad_silu)[0]
    return (
        layer_out,
        tokens_grad,
        conditioning_grad,
        modulation_grad,
        project_grad,
        merge_grad,
        up_grad,
        down_grad,
    )


def solution(mesh):
    return jax.shard_map(
        on_device,
        mesh=mesh,
        in_specs=(
            P("dev", None),
            P(),
            P(),
            P("dev", None),
            P("dev", None),
            P("dev", None),
            P("dev", None),
            P("dev", None),
            P("dev", None),
        ),
        out_specs=(
            P("dev", None),
            P("dev", None),
            P(),
            P("dev", None),
            P("dev", None),
            P("dev", None),
            P("dev", None),
            P("dev", None),
        ),
        check_vma=False,
    )
```

profile of v0, /device:TPU:0, one launch (start us, length us, event | category | flops | bytes accessed | tf_op | source)
XLA Modules:
  0.0 4166.2 jit_solution(7847232623532628059)
XLA Ops:
  13.0 306.8 %all-gather.7.cloned.1.call-done = bf16[3072,9216]{1,0:T(8,128)(2,1)} async-done(((bf16[96,9216]{1,0:T(8,128)(2,1)}), bf16[3072,9216]{1,0:T(8,128)(2,1)}) %all-gather.7.cloned.1.call-update) | async-done | bytes 56623120 | tf_op jit(solution)/shard_map/all_gather | solution.py:141
  319.7 20.9 fusion.179
  347.9 142.7 %all-gather.9.cloned.1.call-done = bf16[3072,4608]{1,0:T(8,128)(2,1)} async-done(((bf16[96,4608]{1,0:T(8,128)(2,1)}), bf16[3072,4608]{1,0:T(8,128)(2,1)}) %all-gather.9.cloned.1.call-update) | async-done | bytes 28311568 | tf_op jit(solution)/shard_map/all_gather | solution.py:142
  624.0 25.8 collective-permute-start.19
  649.9 26.3 collective-permute-start.20
  676.2 20.0 collective-permute-start.21
  715.7 21.0 collective-permute-start.23
  781.4 66.0 %collective-permute-done.29 = bf16[144,1536]{1,0:T(8,128)(2,1)S(1)} collective-permute-done((bf16[144,1536]{1,0:T(8,128)(2,1)S(1)}, bf16[144,1536]{1,0:T(8,128)(2,1)S(1)}, u32[]{:S(2)}, u32[]{:S(2)}) %collective-permute-start.29) | collective-permute-done | bytes 442400 | tf_op jit(solution)/shard_map/ppermute | solution.py:20
  859.3 27.8 collective-permute-done.31
  906.2 65.4 %collective-permute-done.10 = bf16[144,1536]{1,0:T(8,128)(2,1)S(1)} collective-permute-done((bf16[144,1536]{1,0:T(8,128)(2,1)S(1)}, bf16[144,1536]{1,0:T(8,128)(2,1)S(1)}, u32[]{:S(2)}, u32[]{:S(2)}) %collective-permute-start.10) | collective-permute-done | bytes 442400 | tf_op jit(solution)/shard_map/ppermute | solution.py:20
  983.1 58.3 %collective-permute-done.13 = bf16[144,1536]{1,0:T(8,128)(2,1)S(1)} collective-permute-done((bf16[144,1536]{1,0:T(8,128)(2,1)S(1)}, bf16[144,1536]{1,0:T(8,128)(2,1)S(1)}, u32[]{:S(2)}, u32[]{:S(2)}) %collective-permute-start.13) | collective-permute-done | bytes 442400 | tf_op jit(solution)/shard_map/ppermute | solution.py:20
  1041.5 19.6 collective-permute-done.14
  1064.5 164.2 %while.28 = (s32[]{:T(128)}, bf16[24,144,64]{1,2,0:T(8,128)(2,1)S(1)}, f32[24,144]{1,0:T(8,128)}, s32[24]{0:T(128)S(1)}, bf16[144,1536]{1,0:T(8,128)(2,1)S(1)}, ...) while((s32[]{:T(128)}, ...), condition=%wide.region_12.13_spmd.clone, body=%wide.region_9.12_spmd.clone.sunk | while | flops 104799600 | bytes 6301395 | solution.py:191
  1372.0 332.8 %while.29 = (s32[]{:T(128)}, bf16[24,144,64]{1,2,0:T(8,128)(2,1)S(1)}, f32[24,2736,64]{1,2,0:T(8,128)}, f32[24,2736,64]{1,2,0:T(8,128)}, s32[24]{0:T(128)S(1)}, ...) while((s32[]{:T(128)}, ...), condition=%wide.region_19.20_spmd.clone, body=%wide.region_17.19_spmd.clone.sunk | while | flops 256667760 | bytes 15618069 | solution.py:251
  1798.8 20.5 collective-permute-start.65
  1929.5 28.2 fusion.139
  1994.6 18.1 collective-permute-start.46
  2068.0 20.6 fusion.143
  2088.6 97.4 %pad_maximum_fusion = f32[3072,12288]{1,0:T(8,128)} fusion(f32[3072,4608]{1,0:T(8,128)} %fusion.143, f32[3072,6144]{1,0:T(8,128)} %fusion.139, f32[3072,1536]{1,0:T(8,128)} %fusion.135), kind=kLoop, calls=%fused_computation.61 | loop fusion | flops 75497472 | bytes 301989888 | tf_op jit(solution)/shard_map/concatenate | solution.py:280
  2188.9 29.0 fusion.86
  2254.2 105.1 %all-reduce.2 = bf16[4,2,9216]{2,0,1:T(4,128)(2,1)S(1)} all-reduce(f32[4,2,9216]{2,0,1:T(4,128)S(1)} %copy.187), channel_id=1, replica_groups=mesh['dev'=32] {'dev'}, use_global_device_ids=true, to_apply=%region_22.23 | all-reduce | flops 73728 | bytes 442368 | tf_op jit(solution)/shard_map/psum | solution.py:307
  2359.9 39.6 all-gather
  2402.8 1092.8 %reduce-scatter.3.cloned.1.call-done = f32[96,12288]{1,0:T(8,128)} async-done(((f32[3072,12288]{1,0:T(8,128)}), f32[96,12288]{1,0:T(8,128)}) %reduce-scatter.3.cloned.1.call-update) | async-done | bytes 4718608 | tf_op jit(solution)/shard_map/reduce_scatter | solution.py:279
  3503.5 655.4 %reduce-scatter.5.cloned.1.call-done = f32[384,1536]{1,0:T(8,128)} async-done(((f32[12288,1536]{1,0:T(8,128)}), f32[384,1536]{1,0:T(8,128)}) %reduce-scatter.5.cloned.1.call-update) | async-done | bytes 2359312 | tf_op jit(solution)/shard_map/reduce_scatter | solution.py:208
  (824 shorter events, 1164.2 us)
Async XLA Ops:
  7.2 312.5 %all-gather.7.cloned.1.call-start = ((), (), s32[]{:S(2)}) async-start(), calls=%async_computation.2 | async-start | bytes 58392576 | tf_op jit(solution)/shard_map/all_gather | solution.py:141
  7.9 482.6 %all-gather.9.cloned.1.call-start = ((), (), s32[]{:S(2)}) async-start(), calls=%async_computation.3 | async-start | bytes 29196288 | tf_op jit(solution)/shard_map/all_gather | solution.py:142
  8.7 1222.1 %all-gather.11.cloned.1.call-start = ((), (), s32[]{:S(2)}) async-start(), calls=%async_computation.4 | async-start | bytes 9732096 | tf_op jit(solution)/shard_map/all_gather | solution.py:79
  9.4 1238.4 %all-gather.13.cloned.1.call-start = ((), (), s32[]{:S(2)}) async-start(), calls=%async_computation.5 | async-start | bytes 38928384 | tf_op jit(solution)/shard_map/all_gather | solution.py:80
  10.0 1249.3 %all-gather.15.cloned.1.call-start = ((), (), s32[]{:S(2)}) async-start(), calls=%async_computation.6 | async-start | bytes 38928384 | tf_op jit(solution)/shard_map/all_gather | solution.py:81
  10.6 3485.0 %reduce-scatter.3.cloned.1.call-start = ((), (), s32[]{:S(2)}) async-start(), calls=%async_computation.7 | async-start | bytes 155713536 | tf_op jit(solution)/shard_map/reduce_scatter | solution.py:279
  516.3 386.2 %collective-permute-start.35 = (bf16[144,1536]{1,0:T(8,128)(2,1)S(1)}, bf16[144,1536]{1,0:T(8,128)(2,1)S(1)}, u32[]{:S(2)}, u32[]{:S(2)}) collective-permute-start(bf16[144,1536]{1,0:T(8,128)(2,1)S(1)} %get-tuple-element.282), channel_id=1, source_target_pairs={{9,0},{10,1},{11,2},{12,3},{13,4},{14,5},{15,6},{16,7},{17,8},{18,... | collective-permute-start | bytes 1327112 | tf_op jit(solution)/shard_map/ppermute | solution.py:20
  517.6 383.6 %collective-permute-start.34 = (bf16[144,1536]{1,0:T(8,128)(2,1)S(1)}, bf16[144,1536]{1,0:T(8,128)(2,1)S(1)}, u32[]{:S(2)}, u32[]{:S(2)}) collective-permute-start(bf16[144,1536]{1,0:T(8,128)(2,1)S(1)} %get-tuple-element.282), channel_id=1, source_target_pairs={{8,0},{9,1},{10,2},{11,3},{12,4},{13,5},{14,6},{15,7},{16,8},{17,9... | collective-permute-start | bytes 1327112 | tf_op jit(solution)/shard_map/ppermute | solution.py:20
  518.9 380.9 %collective-permute-start.33 = (bf16[144,1536]{1,0:T(8,128)(2,1)S(1)}, bf16[144,1536]{1,0:T(8,128)(2,1)S(1)}, u32[]{:S(2)}, u32[]{:S(2)}) collective-permute-start(bf16[144,1536]{1,0:T(8,128)(2,1)S(1)} %get-tuple-element.282), channel_id=1, source_target_pairs={{7,0},{8,1},{9,2},{10,3},{11,4},{12,5},{13,6},{14,7},{15,8},{16,9}... | collective-permute-start | bytes 1327112 | tf_op jit(solution)/shard_map/ppermute | solution.py:20
  773.8 73.6 %collective-permute-start.29 = (bf16[144,1536]{1,0:T(8,128)(2,1)S(1)}, bf16[144,1536]{1,0:T(8,128)(2,1)S(1)}, u32[]{:S(2)}, u32[]{:S(2)}) collective-permute-start(bf16[144,1536]{1,0:T(8,128)(2,1)S(1)} %get-tuple-element.282), channel_id=1, source_target_pairs={{3,0},{4,1},{5,2},{6,3},{7,4},{8,5},{9,6},{10,7},{11,8},{12,9},{13... | collective-permute-start | bytes 1327112 | tf_op jit(solution)/shard_map/ppermute | solution.py:20
  780.1 77.9 %collective-permute-start.30 = (bf16[144,1536]{1,0:T(8,128)(2,1)S(1)}, bf16[144,1536]{1,0:T(8,128)(2,1)S(1)}, u32[]{:S(2)}, u32[]{:S(2)}) collective-permute-start(bf16[144,1536]{1,0:T(8,128)(2,1)S(1)} %get-tuple-element.282), channel_id=1, source_target_pairs={{4,0},{5,1},{6,2},{7,3},{8,4},{9,5},{10,6},{11,7},{12,8},{13,9},{1... | collective-permute-start | bytes 1327112 | tf_op jit(solution)/shard_map/ppermute | solution.py:20
  887.1 174.1 %collective-permute-start.17 = (bf16[144,1536]{1,0:T(8,128)(2,1)S(1)}, bf16[144,1536]{1,0:T(8,128)(2,1)S(1)}, u32[]{:S(2)}, u32[]{:S(2)}) collective-permute-start(bf16[144,1536]{1,0:T(8,128)(2,1)S(1)} %get-tuple-element.283), channel_id=1, source_target_pairs={{9,0},{10,1},{11,2},{12,3},{13,4},{14,5},{15,6},{16,7},{17,8},{18,... | collective-permute-start | bytes 1327112 | tf_op jit(solution)/shard_map/ppermute | solution.py:20
  898.5 162.6 %collective-permute-start.16 = (bf16[144,1536]{1,0:T(8,128)(2,1)S(1)}, bf16[144,1536]{1,0:T(8,128)(2,1)S(1)}, u32[]{:S(2)}, u32[]{:S(2)}) collective-permute-start(bf16[144,1536]{1,0:T(8,128)(2,1)S(1)} %get-tuple-element.283), channel_id=1, source_target_pairs={{8,0},{9,1},{10,2},{11,3},{12,4},{13,5},{14,6},{15,7},{16,8},{17,9... | collective-permute-start | bytes 1327112 | tf_op jit(solution)/shard_map/ppermute | solution.py:20
  899.8 161.2 %collective-permute-start.15 = (bf16[144,1536]{1,0:T(8,128)(2,1)S(1)}, bf16[144,1536]{1,0:T(8,128)(2,1)S(1)}, u32[]{:S(2)}, u32[]{:S(2)}) collective-permute-start(bf16[144,1536]{1,0:T(8,128)(2,1)S(1)} %get-tuple-element.283), channel_id=1, source_target_pairs={{7,0},{8,1},{9,2},{10,3},{11,4},{12,5},{13,6},{14,7},{15,8},{16,9}... | collective-permute-start | bytes 1327112 | tf_op jit(solution)/shard_map/ppermute | solution.py:20
  904.9 70.3 %collective-permute-start.11 = (bf16[144,1536]{1,0:T(8,128)(2,1)S(1)}, bf16[144,1536]{1,0:T(8,128)(2,1)S(1)}, u32[]{:S(2)}, u32[]{:S(2)}) collective-permute-start(bf16[144,1536]{1,0:T(8,128)(2,1)S(1)} %get-tuple-element.283), channel_id=1, source_target_pairs={{3,0},{4,1},{5,2},{6,3},{7,4},{8,5},{9,6},{10,7},{11,8},{12,9},{13... | collective-permute-start | bytes 1327112 | tf_op jit(solution)/shard_map/ppermute | solution.py:20
  981.8 79.2 %collective-permute-start.14 = (bf16[144,1536]{1,0:T(8,128)(2,1)S(1)}, bf16[144,1536]{1,0:T(8,128)(2,1)S(1)}, u32[]{:S(2)}, u32[]{:S(2)}) collective-permute-start(bf16[144,1536]{1,0:T(8,128)(2,1)S(1)} %get-tuple-element.283), channel_id=1, source_target_pairs={{6,0},{7,1},{8,2},{9,3},{10,4},{11,5},{12,6},{13,7},{14,8},{15,9},... | collective-permute-start | bytes 1327112 | tf_op jit(solution)/shard_map/ppermute | solution.py:20
  1767.4 74.9 %collective-permute-start.61 = (bf16[144,1536]{1,0:T(8,128)(2,1)}, bf16[144,1536]{1,0:T(8,128)(2,1)}, u32[]{:S(2)}, u32[]{:S(2)}) collective-permute-start(bf16[144,1536]{1,0:T(8,128)(2,1)} %copy.220), channel_id=1, source_target_pairs={{2,0},{3,1},{4,2},{5,3},{6,4},{7,5},{8,6},{9,7},{10,8},{11,9},{12,... | collective-permute-start | bytes 1327112 | tf_op jit(solution)/shard_map/ppermute | solution.py:20
  1791.5 78.2 %collective-permute-start.64 = (bf16[144,1536]{1,0:T(8,128)(2,1)}, bf16[144,1536]{1,0:T(8,128)(2,1)}, u32[]{:S(2)}, u32[]{:S(2)}) collective-permute-start(bf16[144,1536]{1,0:T(8,128)(2,1)} %copy.223), channel_id=1, source_target_pairs={{0,2},{1,3},{2,4},{3,5},{4,6},{5,7},{6,8},{7,9},{8,10},{9,11},{10,... | collective-permute-start | bytes 1327112 | tf_op jit(solution)/shard_map/ppermute | solution.py:20
  1798.8 73.0 %collective-permute-start.65 = (bf16[144,1536]{1,0:T(8,128)(2,1)S(1)}, bf16[144,1536]{1,0:T(8,128)(2,1)}, u32[]{:S(2)}, u32[]{:S(2)}) collective-permute-start(bf16[144,1536]{1,0:T(8,128)(2,1)S(1)} %copy.224), channel_id=1, source_target_pairs={{0,3},{1,4},{2,5},{3,6},{4,7},{5,8},{6,9},{7,10},{8,11},{9,12},{10... | collective-permute-start | bytes 1327112 | tf_op jit(solution)/shard_map/ppermute | solution.py:20
  1922.2 72.4 %collective-permute-start.41 = (bf16[144,1536]{1,0:T(8,128)(2,1)}, bf16[144,1536]{1,0:T(8,128)(2,1)}, u32[]{:S(2)}, u32[]{:S(2)}) collective-permute-start(bf16[144,1536]{1,0:T(8,128)(2,1)} %copy.199), channel_id=1, source_target_pairs={{4,0},{5,1},{6,2},{7,3},{8,4},{9,5},{10,6},{11,7},{12,8},{13,9},{1... | collective-permute-start | bytes 1327112 | tf_op jit(solution)/shard_map/ppermute | solution.py:20
  1925.5 87.1 %collective-permute-start.42 = (bf16[144,1536]{1,0:T(8,128)(2,1)}, bf16[144,1536]{1,0:T(8,128)(2,1)}, u32[]{:S(2)}, u32[]{:S(2)}) collective-permute-start(bf16[144,1536]{1,0:T(8,128)(2,1)} %copy.200), channel_id=1, source_target_pairs={{3,0},{4,1},{5,2},{6,3},{7,4},{8,5},{9,6},{10,7},{11,8},{12,9},{13... | collective-permute-start | bytes 1327112 | tf_op jit(solution)/shard_map/ppermute | solution.py:20
  1926.8 90.0 %collective-permute-start.43 = (bf16[144,1536]{1,0:T(8,128)(2,1)}, bf16[144,1536]{1,0:T(8,128)(2,1)}, u32[]{:S(2)}, u32[]{:S(2)}) collective-permute-start(bf16[144,1536]{1,0:T(8,128)(2,1)} %copy.201), channel_id=1, source_target_pairs={{2,0},{3,1},{4,2},{5,3},{6,4},{7,5},{8,6},{9,7},{10,8},{11,9},{12,... | collective-permute-start | bytes 1327112 | tf_op jit(solution)/shard_map/ppermute | solution.py:20
  1928.1 91.4 %collective-permute-start.44 = (bf16[144,1536]{1,0:T(8,128)(2,1)}, bf16[144,1536]{1,0:T(8,128)(2,1)}, u32[]{:S(2)}, u32[]{:S(2)}) collective-permute-start(bf16[144,1536]{1,0:T(8,128)(2,1)} %copy.202), channel_id=1, source_target_pairs={{1,0},{2,1},{3,2},{4,3},{5,4},{6,5},{7,6},{8,7},{9,8},{10,9},{11,1... | collective-permute-start | bytes 1327112 | tf_op jit(solution)/shard_map/ppermute | solution.py:20
  2186.0 1972.8 %reduce-scatter.5.cloned.1.call-start = ((), (), s32[]{:S(2)}) async-start(), calls=%async_computation.8 | async-start | bytes 77856768 | tf_op jit(solution)/shard_map/reduce_scatter | solution.py:208
  (131 other events, 9052.0 us)
Sparse Core Ops, SparseCore 0:
  10.9 308.7 all-gather.6
  322.6 167.8 all-gather.8
  493.4 105.1 all-gather.10
  601.4 330.3 all-gather.12
  934.6 275.7 all-gather.14
  2186.2 1309.3 reduce-scatter.2
  3503.7 655.1 reduce-scatter.4
where the time goes:
time: 4190 us; the launch traced here: 4170 us
  waiting for transfers between devices  2590 us (62%)
  matrix products  586 us (14%)
  starting transfers between devices  366 us (9%)
  local copies, waits for them, and re-layouts  237 us (6%)
  other arithmetic  152 us (4%)
  blocking collectives  145 us (3%)
  loops' own time  78.1 us (2%)
    reduce_scatter x1, waiting for transfers between devices, on_device(): lax.psum_scatter(jnp.concatenate([term_rows(attended_split, grad_merged),...  1090 us
    reduce_scatter x1, waiting for transfers between devices, on_device(): lax.psum_scatter(term_rows(activated_split, grad_lowered), 'dev', scatter...  655 us
    ppermute x72, waiting for transfers between devices, passed_along(): return lax.ppermute(x, axis, pairs)  385 us
    ppermute x72, starting transfers between devices, passed_along(): return lax.ppermute(x, axis, pairs)  365 us
    all_gather x1, waiting for transfers between devices, on_device(): lax.all_gather(modulation_weight, 'dev', axis=0, tiled=True)  307 us
    all_gather x1, waiting for transfers between devices, on_device(): lax.all_gather(project_weight, 'dev', axis=0, tiled=True)  143 us
    psum x1, blocking collectives, on_device(): lax.psum(local_table.reshape(seq_count, 2, 6 * width), 'dev')  105 us
    concatenate x1, other arithmetic, on_device(): jnp.concatenate([term_rows(attended_split, grad_merged), term_rows(hidden...  97.4 us
  transfers between devices with their start and end apart: 79, of which 31 were waited for; matrix products, arithmetic and copies ran while one was open for 11% of the time, Pallas kernels for 0%

commit v1 on v0

--- a/solution.py
+++ b/solution.py
@@ -12,6 +12,18 @@
 EPSILON = 1e-06
 CONTRACT_LAST = (((1,), (1,)), ((), ()))
 CONTRACT_FIRST = (((0,), (0,)), ((), ()))
+
+
+def gather_by_bits(x, axis, dim):
+    ways, here, step = (lax.axis_size(axis), lax.axis_index(axis), x.shape[dim])
+    line, have = (x, 1)
+    while have < ways:
+        line = jnp.concatenate(
+            [line, lax.ppermute(line, axis, [(d, (d - have) % ways) for d in range(ways)])],
+            axis=dim,
+        )
+        have = 2 * have
+    return jnp.roll(line, here * step, axis=dim)
 
 
 def passed_along(x, axis, by):
@@ -139,7 +151,7 @@
     silu_part = lax.dynamic_slice_in_dim(silu_low, feature_start, shard_rows, 1)
     mod_full, project_full = (
         lax.all_gather(modulation_weight, "dev", axis=0, tiled=True),
-        lax.all_gather(project_weight, "dev", axis=0, tiled=True),
+        gather_by_bits(project_weight, "dev", 0),
     )
     mod_table = jnp.einsum(
         "sd,jdc->sjc",

time: 4190 us -> 5040 us (1.20)
  waiting for transfers between devices: 2590 us -> 3330 us
  starting transfers between devices: 366 us -> 430 us
  blocking collectives: 145 us -> 91.7 us
  local copies, waits for them, and re-layouts: 237 us -> 290 us
    ppermute x0 -> x5, waiting for transfers between devices: none -> 1150 us  [gather_by_bits(): lax.ppermute(line, axis, [(d, (d - have) % ways) for d in range(ways)])]
    all_gather x1, waiting for transfers between devices: 307 us -> 0.01 us  [on_device(): lax.all_gather(modulation_weight, 'dev', axis=0, tiled=True)]
    all_gather x1, waiting for transfers between devices: 143 us -> 0.01 us  [on_device(): project_again = lax.all_gather(project_weight, 'dev', axis=0, tiled=True)]
    ppermute x72, starting transfers between devices: 365 us -> 423 us  [passed_along(): return lax.ppermute(x, axis, pairs)]
    psum x1, blocking collectives: 105 us -> 52.7 us  [on_device(): lax.psum(local_table.reshape(seq_count, 2, 6 * width), 'dev')]
  transfers between devices with their start and end apart: 79 -> 84, of which waited for: 31 -> 30; matrix products, arithmetic and copies ran while one was open for 11% -> 21% of each run, Pallas kernels for 0% -> 0%
where the time goes in v1:
time: 5040 us; the launch traced here: 5020 us
  waiting for transfers between devices  3330 us (66%)
  matrix products  628 us (12%)
  starting transfers between devices  430 us (9%)
  local copies, waits for them, and re-layouts  290 us (6%)
  other arithmetic  160 us (3%)
  blocking collectives  91.7 us (2%)
  loops' own time  76.6 us (2%)
    ppermute x5, waiting for transfers between devices, gather_by_bits(): lax.ppermute(line, axis, [(d, (d - have) % ways) for d in range(ways)])  1150 us
    reduce_scatter x1, waiting for transfers between devices, on_device(): lax.psum_scatter(jnp.concatenate([term_rows(attended_split, grad_merged),...  1090 us
    reduce_scatter x1, waiting for transfers between devices, on_device(): lax.psum_scatter(term_rows(activated_split, grad_lowered), 'dev', scatter...  656 us
    ppermute x72, waiting for transfers between devices, passed_along(): return lax.ppermute(x, axis, pairs)  428 us
    ppermute x72, starting transfers between devices, passed_along(): return lax.ppermute(x, axis, pairs)  423 us
  transfers between devices with their start and end apart: 84, of which 30 were waited for; matrix products, arithmetic and copies ran while one was open for 21% of the time, Pallas kernels for 0%

profile of v1, /device:TPU:0, one launch (start us, length us, event | category | flops | bytes accessed | tf_op | source)
XLA Modules:
  0.0 5018.3 jit_solution(15408323663334059411)
XLA Ops:
  34.0 67.6 %collective-permute-done.1 = bf16[192,4608]{1,0:T(8,128)(2,1)S(1)} collective-permute-done((bf16[192,4608]{1,0:T(8,128)(2,1)S(1)}, bf16[192,4608]{1,0:T(8,128)(2,1)S(1)}, u32[]{:S(2)}, u32[]{:S(2)}) %collective-permute-start.1) | collective-permute-done | bytes 1769504 | tf_op jit(solution)/shard_map/ppermute | solution.py:22
  101.8 152.5 %collective-permute-done.2 = bf16[384,4608]{1,0:T(8,128)(2,1)S(1)} collective-permute-done((bf16[384,4608]{1,0:T(8,128)(2,1)S(1)}, bf16[384,4608]{1,0:T(8,128)(2,1)S(1)}, u32[]{:S(2)}, u32[]{:S(2)}) %collective-permute-start.2) | collective-permute-done | bytes 3538976 | tf_op jit(solution)/shard_map/ppermute | solution.py:22
  261.2 300.6 %collective-permute-done.3 = bf16[768,4608]{1,0:T(8,128)(2,1)} collective-permute-done((bf16[768,4608]{1,0:T(8,128)(2,1)S(1)}, bf16[768,4608]{1,0:T(8,128)(2,1)}, u32[]{:S(2)}, u32[]{:S(2)}) %collective-permute-start.3) | collective-permute-done | bytes 7077920 | tf_op jit(solution)/shard_map/ppermute | solution.py:22
  575.9 611.1 %collective-permute-done.4 = bf16[1536,4608]{1,0:T(8,128)(2,1)} collective-permute-done((bf16[1536,4608]{1,0:T(8,128)(2,1)}, bf16[1536,4608]{1,0:T(8,128)(2,1)}, u32[]{:S(2)}, u32[]{:S(2)}) %collective-permute-start.4) | collective-permute-done | bytes 14155808 | tf_op jit(solution)/shard_map/ppermute | solution.py:22
  1346.2 33.3 collective-permute-start.6
  1379.5 29.3 collective-permute-start.7
  1532.6 48.4 collective-permute-done.19
  1582.3 25.5 collective-permute-done.20
  1609.2 45.7 collective-permute-done.21
  1679.4 49.5 collective-permute-done.38
  1728.9 76.4 %collective-permute-done.39 = bf16[144,1536]{1,0:T(8,128)(2,1)S(1)} collective-permute-done((bf16[144,1536]{1,0:T(8,128)(2,1)S(1)}, bf16[144,1536]{1,0:T(8,128)(2,1)S(1)}, u32[]{:S(2)}, u32[]{:S(2)}) %collective-permute-start.39) | collective-permute-done | bytes 442400 | tf_op jit(solution)/shard_map/ppermute | solution.py:32
  1816.0 163.7 %while.28 = (s32[]{:T(128)}, bf16[24,144,64]{1,2,0:T(8,128)(2,1)S(1)}, f32[24,144]{1,0:T(8,128)}, s32[24]{0:T(128)S(1)}, bf16[144,1536]{1,0:T(8,128)(2,1)S(1)}, ...) while((s32[]{:T(128)}, ...), condition=%wide.region_12.13_spmd.clone, body=%wide.region_9.12_spmd.clone.sunk | while | flops 104799600 | bytes 6301395 | solution.py:203
  2132.3 345.8 %while.29 = (s32[]{:T(128)}, bf16[24,144,64]{1,2,0:T(8,128)(2,1)}, f32[24,2736,64]{1,2,0:T(8,128)}, f32[24,2736,64]{1,2,0:T(8,128)}, s32[24]{0:T(128)S(1)}, /*in...) while((s32[]{:T(128)}, bf16[24,144,64]{1,2,0:T(8,128)(2,1)}, ...), condition=%wide.region_19.20_spmd.clone, body=%wide.region_17.19_spmd.clone.sunk | while | flops 256667760 | bytes 15595029 | solution.py:263
  2496.2 82.1 %collective-permute-start.76 = (bf16[144,1536]{1,0:T(8,128)(2,1)}, bf16[144,1536]{1,0:T(8,128)(2,1)}, u32[]{:S(2)}, u32[]{:S(2)}) collective-permute-start(bf16[144,1536]{1,0:T(8,128)(2,1)} %copy.230), channel_id=1, source_target_pairs={{0,9},{1,10},{2,11},{3,12},{4,13},{5,14},{6,15},{7,16},{8,17},{9,1... | collective-permute-start | bytes 1327112 | tf_op jit(solution)/shard_map/ppermute | solution.py:32
  2580.5 33.7 collective-permute-start.75
  2795.7 28.1 fusion.133
  2904.5 47.1 collective-permute-done.42
  2956.2 21.8 fusion.137
  2978.0 97.8 %pad_maximum_fusion = f32[3072,12288]{1,0:T(8,128)} fusion(f32[3072,4608]{1,0:T(8,128)} %fusion.137, f32[3072,6144]{1,0:T(8,128)} %fusion.133, f32[3072,1536]{1,0:T(8,128)} %fusion.129), kind=kLoop, calls=%fused_computation.61 | loop fusion | flops 75497472 | bytes 301989888 | tf_op jit(solution)/shard_map/concatenate | solution.py:292
  3078.7 40.2 fusion.80
  3159.5 52.7 %all-reduce.2 = bf16[4,2,9216]{2,0,1:T(4,128)(2,1)S(1)} all-reduce(f32[4,2,9216]{2,0,1:T(4,128)S(1)} %copy.187), channel_id=1, replica_groups=mesh['dev'=32] {'dev'}, use_global_device_ids=true, to_apply=%region_22.23 | all-reduce | flops 73728 | bytes 442368 | tf_op jit(solution)/shard_map/psum | solution.py:319
  3212.7 39.0 all-gather
  3255.1 1092.1 %reduce-scatter.3.cloned.1.call-done = f32[96,12288]{1,0:T(8,128)} async-done(((f32[3072,12288]{1,0:T(8,128)}), f32[96,12288]{1,0:T(8,128)}) %reduce-scatter.3.cloned.1.call-update) | async-done | bytes 4718608 | tf_op jit(solution)/shard_map/reduce_scatter | solution.py:291
  4355.1 655.9 %reduce-scatter.5.cloned.1.call-done = f32[384,1536]{1,0:T(8,128)} async-done(((f32[12288,1536]{1,0:T(8,128)}), f32[384,1536]{1,0:T(8,128)}) %reduce-scatter.5.cloned.1.call-update) | async-done | bytes 2359312 | tf_op jit(solution)/shard_map/reduce_scatter | solution.py:220
  (862 shorter events, 1294.5 us)
Async XLA Ops:
  7.2 1213.3 %all-gather.7.cloned.1.call-start = ((), (), s32[]{:S(2)}) async-start(), calls=%async_computation.2 | async-start | bytes 58392576 | tf_op jit(solution)/shard_map/all_gather | solution.py:153
  7.9 1974.3 %all-gather.9.cloned.1.call-start = ((), (), s32[]{:S(2)}) async-start(), calls=%async_computation.3 | async-start | bytes 9732096 | tf_op jit(solution)/shard_map/all_gather | solution.py:91
  8.7 1989.0 %all-gather.11.cloned.1.call-start = ((), (), s32[]{:S(2)}) async-start(), calls=%async_computation.4 | async-start | bytes 38928384 | tf_op jit(solution)/shard_map/all_gather | solution.py:92
  9.4 2003.1 %all-gather.13.cloned.1.call-start = ((), (), s32[]{:S(2)}) async-start(), calls=%async_computation.5 | async-start | bytes 38928384 | tf_op jit(solution)/shard_map/all_gather | solution.py:93
  10.0 3113.1 %all-gather.15.cloned.1.call-start = ((), (), s32[]{:S(2)}) async-start(), calls=%async_computation.6 | async-start | bytes 29196288 | tf_op jit(solution)/shard_map/all_gather | solution.py:288
  101.8 152.6 %collective-permute-start.2 = (bf16[384,4608]{1,0:T(8,128)(2,1)S(1)}, bf16[384,4608]{1,0:T(8,128)(2,1)S(1)}, u32[]{:S(2)}, u32[]{:S(2)}) collective-permute-start(bf16[384,4608]{1,0:T(8,128)(2,1)S(1)} %pad_maximum_fusion.2), channel_id=1, source_target_pairs={{0,28},{1,29},{2,30},{3,31},{4,0},{5,1},{6,2},{7,3},{8,4},{9,5},{1... | collective-permute-start | bytes 10616840 | tf_op jit(solution)/shard_map/ppermute | solution.py:22
  255.0 306.8 %collective-permute-start.3 = (bf16[768,4608]{1,0:T(8,128)(2,1)S(1)}, bf16[768,4608]{1,0:T(8,128)(2,1)}, u32[]{:S(2)}, u32[]{:S(2)}) collective-permute-start(bf16[768,4608]{1,0:T(8,128)(2,1)S(1)} %pad_maximum_fusion.1), channel_id=1, source_target_pairs={{0,24},{1,25},{2,26},{3,27},{4,28},{5,29},{6,30},{7,31},{8,0},{9,1... | collective-permute-start | bytes 21233672 | tf_op jit(solution)/shard_map/ppermute | solution.py:22
  570.8 616.2 %collective-permute-start.4 = (bf16[1536,4608]{1,0:T(8,128)(2,1)}, bf16[1536,4608]{1,0:T(8,128)(2,1)}, u32[]{:S(2)}, u32[]{:S(2)}) collective-permute-start(bf16[1536,4608]{1,0:T(8,128)(2,1)} %get-tuple-element.275), channel_id=1, source_target_pairs={{0,16},{1,17},{2,18},{3,19},{4,20},{5,21},{6,22},{7,23},{8,24},{9,... | collective-permute-start | bytes 42467336 | tf_op jit(solution)/shard_map/ppermute | solution.py:22
  570.8 3776.3 %reduce-scatter.3.cloned.1.call-start = ((), (), s32[]{:S(2)}) async-start(), calls=%async_computation.7 | async-start | bytes 155713536 | tf_op jit(solution)/shard_map/reduce_scatter | solution.py:291
  1321.9 87.0 %collective-permute-start.29 = (bf16[144,1536]{1,0:T(8,128)(2,1)S(1)}, bf16[144,1536]{1,0:T(8,128)(2,1)S(1)}, u32[]{:S(2)}, u32[]{:S(2)}) collective-permute-start(bf16[144,1536]{1,0:T(8,128)(2,1)S(1)} %get-tuple-element.288), channel_id=1, source_target_pairs={{0,3},{1,4},{2,5},{3,6},{4,7},{5,8},{6,9},{7,10},{8,11},{9,12},{10... | collective-permute-start | bytes 1327112 | tf_op jit(solution)/shard_map/ppermute | solution.py:32
  1325.1 92.2 %collective-permute-start.30 = (bf16[144,1536]{1,0:T(8,128)(2,1)S(1)}, bf16[144,1536]{1,0:T(8,128)(2,1)S(1)}, u32[]{:S(2)}, u32[]{:S(2)}) collective-permute-start(bf16[144,1536]{1,0:T(8,128)(2,1)S(1)} %get-tuple-element.288), channel_id=1, source_target_pairs={{0,2},{1,3},{2,4},{3,5},{4,6},{5,7},{6,8},{7,9},{8,10},{9,11},{10,... | collective-permute-start | bytes 1327112 | tf_op jit(solution)/shard_map/ppermute | solution.py:32
  1344.7 80.4 %collective-permute-start.31 = (bf16[144,1536]{1,0:T(8,128)(2,1)S(1)}, bf16[144,1536]{1,0:T(8,128)(2,1)S(1)}, u32[]{:S(2)}, u32[]{:S(2)}) collective-permute-start(bf16[144,1536]{1,0:T(8,128)(2,1)S(1)} %get-tuple-element.288), channel_id=1, source_target_pairs={{0,1},{1,2},{2,3},{3,4},{4,5},{5,6},{6,7},{7,8},{8,9},{9,10},{10,1... | collective-permute-start | bytes 1327112 | tf_op jit(solution)/shard_map/ppermute | solution.py:32
  1346.2 99.7 %collective-permute-start.6 = (bf16[144,1536]{1,0:T(8,128)(2,1)S(1)}, bf16[144,1536]{1,0:T(8,128)(2,1)S(1)}, u32[]{:S(2)}, u32[]{:S(2)}) collective-permute-start(bf16[144,1536]{1,0:T(8,128)(2,1)S(1)} %get-tuple-element.289), channel_id=1, source_target_pairs={{0,8},{1,9},{2,10},{3,11},{4,12},{5,13},{6,14},{7,15},{8,16},{9,17... | collective-permute-start | bytes 1327112 | tf_op jit(solution)/shard_map/ppermute | solution.py:32
  1498.0 83.0 %collective-permute-start.19 = (bf16[144,1536]{1,0:T(8,128)(2,1)S(1)}, bf16[144,1536]{1,0:T(8,128)(2,1)S(1)}, u32[]{:S(2)}, u32[]{:S(2)}) collective-permute-start(bf16[144,1536]{1,0:T(8,128)(2,1)S(1)} %get-tuple-element.289), channel_id=1, source_target_pairs={{6,0},{7,1},{8,2},{9,3},{10,4},{11,5},{12,6},{13,7},{14,8},{15,9},... | collective-permute-start | bytes 1327112 | tf_op jit(solution)/shard_map/ppermute | solution.py:32
  1520.0 87.8 %collective-permute-start.20 = (bf16[144,1536]{1,0:T(8,128)(2,1)S(1)}, bf16[144,1536]{1,0:T(8,128)(2,1)S(1)}, u32[]{:S(2)}, u32[]{:S(2)}) collective-permute-start(bf16[144,1536]{1,0:T(8,128)(2,1)S(1)} %get-tuple-element.289), channel_id=1, source_target_pairs={{7,0},{8,1},{9,2},{10,3},{11,4},{12,5},{13,6},{14,7},{15,8},{16,9}... | collective-permute-start | bytes 1327112 | tf_op jit(solution)/shard_map/ppermute | solution.py:32
  1521.6 133.3 %collective-permute-start.21 = (bf16[144,1536]{1,0:T(8,128)(2,1)S(1)}, bf16[144,1536]{1,0:T(8,128)(2,1)S(1)}, u32[]{:S(2)}, u32[]{:S(2)}) collective-permute-start(bf16[144,1536]{1,0:T(8,128)(2,1)S(1)} %get-tuple-element.289), channel_id=1, source_target_pairs={{8,0},{9,1},{10,2},{11,3},{12,4},{13,5},{14,6},{15,7},{16,8},{17,9... | collective-permute-start | bytes 1327112 | tf_op jit(solution)/shard_map/ppermute | solution.py:32
  1522.9 136.7 %collective-permute-start.22 = (bf16[144,1536]{1,0:T(8,128)(2,1)S(1)}, bf16[144,1536]{1,0:T(8,128)(2,1)S(1)}, u32[]{:S(2)}, u32[]{:S(2)}) collective-permute-start(bf16[144,1536]{1,0:T(8,128)(2,1)S(1)} %get-tuple-element.289), channel_id=1, source_target_pairs={{9,0},{10,1},{11,2},{12,3},{13,4},{14,5},{15,6},{16,7},{17,8},{18,... | collective-permute-start | bytes 1327112 | tf_op jit(solution)/shard_map/ppermute | solution.py:32
  1531.3 129.7 %collective-permute-start.32 = (bf16[144,1536]{1,0:T(8,128)(2,1)S(1)}, bf16[144,1536]{1,0:T(8,128)(2,1)S(1)}, u32[]{:S(2)}, u32[]{:S(2)}) collective-permute-start(bf16[144,1536]{1,0:T(8,128)(2,1)S(1)} %get-tuple-element.288), channel_id=1, source_target_pairs={{1,0},{2,1},{3,2},{4,3},{5,4},{6,5},{7,6},{8,7},{9,8},{10,9},{11,1... | collective-permute-start | bytes 1327112 | tf_op jit(solution)/shard_map/ppermute | solution.py:32
  1581.0 81.3 %collective-permute-start.33 = (bf16[144,1536]{1,0:T(8,128)(2,1)S(1)}, bf16[144,1536]{1,0:T(8,128)(2,1)S(1)}, u32[]{:S(2)}, u32[]{:S(2)}) collective-permute-start(bf16[144,1536]{1,0:T(8,128)(2,1)S(1)} %get-tuple-element.288), channel_id=1, source_target_pairs={{2,0},{3,1},{4,2},{5,3},{6,4},{7,5},{8,6},{9,7},{10,8},{11,9},{12,... | collective-permute-start | bytes 1327112 | tf_op jit(solution)/shard_map/ppermute | solution.py:32
  1663.7 141.6 %collective-permute-start.39 = (bf16[144,1536]{1,0:T(8,128)(2,1)S(1)}, bf16[144,1536]{1,0:T(8,128)(2,1)S(1)}, u32[]{:S(2)}, u32[]{:S(2)}) collective-permute-start(bf16[144,1536]{1,0:T(8,128)(2,1)S(1)} %get-tuple-element.288), channel_id=1, source_target_pairs={{8,0},{9,1},{10,2},{11,3},{12,4},{13,5},{14,6},{15,7},{16,8},{17,9... | collective-permute-start | bytes 1327112 | tf_op jit(solution)/shard_map/ppermute | solution.py:32
  1675.1 137.6 %collective-permute-start.40 = (bf16[144,1536]{1,0:T(8,128)(2,1)S(1)}, bf16[144,1536]{1,0:T(8,128)(2,1)S(1)}, u32[]{:S(2)}, u32[]{:S(2)}) collective-permute-start(bf16[144,1536]{1,0:T(8,128)(2,1)S(1)} %get-tuple-element.288), channel_id=1, source_target_pairs={{9,0},{10,1},{11,2},{12,3},{13,4},{14,5},{15,6},{16,7},{17,8},{18,... | collective-permute-start | bytes 1327112 | tf_op jit(solution)/shard_map/ppermute | solution.py:32
  2496.2 147.1 %collective-permute-start.76 = (bf16[144,1536]{1,0:T(8,128)(2,1)}, bf16[144,1536]{1,0:T(8,128)(2,1)}, u32[]{:S(2)}, u32[]{:S(2)}) collective-permute-start(bf16[144,1536]{1,0:T(8,128)(2,1)} %copy.230), channel_id=1, source_target_pairs={{0,9},{1,10},{2,11},{3,12},{4,13},{5,14},{6,15},{7,16},{8,17},{9,1... | collective-permute-start | bytes 1327112 | tf_op jit(solution)/shard_map/ppermute | solution.py:32
  2773.0 78.8 %collective-permute-start.55 = (bf16[144,1536]{1,0:T(8,128)(2,1)}, bf16[144,1536]{1,0:T(8,128)(2,1)}, u32[]{:S(2)}, u32[]{:S(2)}) collective-permute-start(bf16[144,1536]{1,0:T(8,128)(2,1)} %copy.208), channel_id=1, source_target_pairs={{0,6},{1,7},{2,8},{3,9},{4,10},{5,11},{6,12},{7,13},{8,14},{9,15},... | collective-permute-start | bytes 1327112 | tf_op jit(solution)/shard_map/ppermute | solution.py:32
  3075.9 1935.1 %reduce-scatter.5.cloned.1.call-start = ((), (), s32[]{:S(2)}) async-start(), calls=%async_computation.8 | async-start | bytes 77856768 | tf_op jit(solution)/shard_map/reduce_scatter | solution.py:220
  (142 other events, 6011.7 us)
Sparse Core Ops, SparseCore 0:
  10.9 548.7 all-gather.6
  562.6 686.3 all-gather.8
  1251.9 308.6 all-gather.10
  1563.3 382.0 all-gather.12
  1948.1 165.7 all-gather.14
  3076.0 1271.0 reduce-scatter.2
  4355.3 655.6 reduce-scatter.4
